TPU v7x, 32 devices: a whole 2x2x4 slice. The times are simulated.
32 devices in a mesh: grp: 2 (over y), col: 4 (over z), row: 2 (over x), dir: 2 (over core).
Axes of the slice: x: 2, y: 2, z: 4, core: 2. Of those that a mesh axis runs over, the one named last changes fastest.
Arguments:
- slopes_in: bfloat16 [512, 8192], P(None, ('grp', 'col')), parts along dimension 1, may hold values from -6 to 6
- basis_left: bfloat16 [12, 16, 256, 256], P(('row', 'dir'), 'col'), may hold values from -0.09375 to 0.09375
- basis_right: bfloat16 [12, 16, 256, 256], P(('row', 'dir'), 'col'), may hold values from -0.375 to 0.375
- rank_blocks: int32 [12, 16], P(('row', 'dir'), 'col'), may hold values from 1 to 4
- tile_owner: int32 [16], replicated, may hold values from 0 to 15, each once
- footprint: int32 [4, 4, 4, 2048], P(('row', 'dir')), may hold values from 0 to 767
- trace_weight: float32 [4, 4, 4, 2048], P(('row', 'dir')), may hold values from 0 to 0.5
- fitting: bfloat16 [2048, 4096], P(None, 'col'), may hold values from -0.125 to 0.125
Outputs:
- commands: bfloat16 [4, 1024, 4096], P(('row', 'dir'), 'grp', 'col'), parts along dimension 1
There are 2 independent parts, one for each index of `grp`. A program takes and returns all parts, laid end to end along the dimension named above; an argument that names none is the same for every part. Nothing has to cross between parts.
Inputs may be any that keep to these rules, and one draw needn't show every extreme that they name: rank_blocks[i, k] is the number of leading blocks of 64 columns of tile (i, k) that are live. `tile_owner`: each slope block appears in exactly one tile slot. `footprint`: indices into one layer's points.
All inputs are finite; a program needn't handle non-finite values.
Results may differ from a plain program's by a relative error of at most 0.0064.
Values may be sent and summed in bfloat16 or wider, within the bound.
No kernel may reach another device: no remote copies, remote signals or barrier semaphores. Data moves between devices by JAX's collectives and lax.ppermute only.
A program may use at most 128 MiB of HBM per device.

v0:
```python
import jax
import jax.numpy as jnp
from jax import lax
from jax.sharding import PartitionSpec as P

RB = 64


def shards(
    slopes_in, basis_left, basis_right, rank_blocks, tile_owner, footprint, trace_weight, fitting
):
    frames = slopes_in.shape[0]
    tile_size = basis_left.shape[2]
    rows_here = basis_left.shape[0]
    slots_here = basis_left.shape[1]
    rank_cols = basis_left.shape[3]
    owners = lax.dynamic_slice_in_dim(tile_owner, lax.axis_index("col") * slots_here, slots_here, 0)
    share = frames // lax.axis_size(("row", "dir"))
    mine = lax.dynamic_slice_in_dim(slopes_in, lax.axis_index(("row", "dir")) * share, share, 0)
    partial_value = lax.all_gather(mine, "col", axis=1, tiled=True)
    picked = jnp.take(partial_value.reshape(share, -1, tile_size), owners, axis=1)
    chosen = lax.all_gather(picked, ("row", "dir"), axis=0, tiled=True)
    columns = jnp.arange(rank_cols, dtype=jnp.int32) // RB
    live = columns[None, None, None, :] < rank_blocks[:, :, None, None]
    frame_share = frames // lax.axis_size("col")
    coeffs = jnp.einsum("fkn,iknr->ikfr", chosen, basis_right, preferred_element_type=jnp.float32)
    coeffs = jnp.where(live, coeffs, 0.0).astype(jnp.bfloat16)
    summed = jnp.einsum("ikfr,iknr->fin", coeffs, basis_left, preferred_element_type=jnp.float32)
    layer_block = lax.psum_scatter(
        summed.reshape(lax.axis_size("col") * frame_share, rows_here * tile_size),
        "col",
        scatter_dimension=0,
        tiled=True,
    ).astype(jnp.bfloat16)
    layers = lax.all_gather(layer_block, ("row", "dir"), axis=1, tiled=True)
    layer_count = footprint.shape[1]
    pupil_count = footprint.shape[3]
    per_layer = layers.shape[1] // layer_count
    shifts = (jnp.arange(layer_count, dtype=jnp.int32) * per_layer)[:, None, None]
    flat = (footprint[0] + shifts).reshape(-1)
    values = (
        jnp.take(layers, flat, axis=1)
        .astype(jnp.float32)
        .reshape(frame_share, layer_count, 4, pupil_count)
    )
    pupil = jnp.sum(values * trace_weight[0][None], axis=(1, 2)).astype(jnp.bfloat16)
    commands = jnp.dot(
        lax.all_gather(pupil, "col", axis=0, tiled=True),
        fitting,
        preferred_element_type=jnp.float32,
    )
    return commands.astype(jnp.bfloat16)[None]


def solution(mesh):
    placed = (
        P(None, ("grp", "col")),
        P(("row", "dir"), "col", None, None),
        P(("row", "dir"), "col", None, None),
        P(("row", "dir"), "col"),
        P(),
        P(("row", "dir"), None, None, None),
        P(("row", "dir"), None, None, None),
        P(None, "col"),
    )
    return jax.shard_map(
        shards,
        mesh=mesh,
        in_specs=placed,
        out_specs=P(("row", "dir"), "grp", "col"),
        check_vma=False,
    )
```

profile of v0, /device:TPU:0, one launch (start us, length us, event | category | flops | bytes accessed | tf_op | source)
XLA Modules:
  0.0 293.8 jit_solution(6185712206535708235)
XLA Ops:
  6.5 0.0 copy-start
  6.5 0.0 copy-start.1
  6.5 0.0 copy-start.3
  6.5 0.0 all-gather.4.cloned.1.call-start
  6.6 1.1 constant_dynamic-slice_fusion
  7.7 0.8 copy.14
  8.5 0.0 all-gather.4.cloned.1.call-update
  8.5 0.0 all-gather.6.cloned.1.call-start
  8.6 0.7 compare_and_fusion.1
  9.3 30.3 %all-gather.4.cloned.1.call-done = bf16[128,4096]{0,1:T(8,128)(2,1)} async-done(((bf16[128,1024]{0,1:T(8,128)(2,1)}), bf16[128,4096]{0,1:T(8,128)(2,1)}) %all-gather.4.cloned.1.call-update) | async-done | bytes 1048592 | tf_op jit(solution)/shard_map/all_gather | solution.py:20
  39.6 1.5 copy.12
  41.1 0.6 gather_fusion
  41.7 0.8 select_bitcast_fusion
  42.5 0.0 all-gather.6.cloned.1.call-update
  42.5 0.0 reduce-scatter.2.cloned.1.call-start
  42.6 0.1 add.67
  42.7 0.2 add.75
  42.9 0.0 copy-done.1
  42.9 0.2 squeeze.6
  43.1 0.0 copy-done.3
  43.1 0.1 broadcast_compare_fusion
  43.1 15.6 %all-gather.6.cloned.1.call-done = bf16[512,4,256]{2,0,1:T(8,128)(2,1)} async-done(((bf16[128,4,256]{2,0,1:T(8,128)(2,1)}), bf16[512,4,256]{2,0,1:T(8,128)(2,1)}) %all-gather.6.cloned.1.call-update) | async-done | bytes 1048592 | tf_op jit(solution)/shard_map/all_gather | solution.py:22
  58.8 0.0 copy-done
  58.8 4.7 %fusion.1 = f32[3,512,256,1]{1,2,3,0:T(8,128)} fusion(bf16[3,4,256,256]{3,2,1,0:T(8,128)(2,1)S(1)} %copy-done, pred[3,4,256]{2,1,0:T(4,128)(4,1)S(1)} %broadcast_compare_fusion, bf16[3,4,256,256]{3,2,1,0:T(8,128)(2,1)} %param.10, bf16[512,4,256]{2,0,1:T(8,128)(2,1)} %all-gather.6.cloned.1.call-done), kind=kOutput, calls=%fused_computation.5 | convolution fusion | flops 1613758464 | bytes 5770240 | tf_op jit(solution)/shard_map/ikfr,iknr->fin/dot_general | solution.py:28
  63.4 0.0 reduce-scatter.2.cloned.1.call-update
  63.5 0.0 all-gather.8.cloned.1.call-start
  63.5 0.2 compare_select_fusion
  63.7 0.2 compare_and_fusion
  63.9 35.2 %reduce-scatter.2.cloned.1.call-done = f32[128,768]{0,1:T(8,128)} async-done(((f32[512,768]{0,1:T(8,128)}), f32[128,768]{0,1:T(8,128)}) %reduce-scatter.2.cloned.1.call-update) | async-done | bytes 393232 | tf_op jit(solution)/shard_map/reduce_scatter | solution.py:29
  99.1 1.0 convert_element_type.17
  100.1 8.6 %all_gather.14 = bf16[128,3072]{0,1:T(8,128)(2,1)S(1)} all-gather(bf16[128,768]{0,1:T(8,128)(2,1)S(1)} %convert_element_type.17), channel_id=1, replica_groups=mesh['grp'=2,'col'=4,'row'=2,'dir'=2] {'row','dir'}, dimensions={1}, use_global_device_ids=true | all-gather | bytes 983040 | tf_op jit(solution)/shard_map/all_gather | solution.py:35
  108.6 0.0 copy-start.2
  108.6 114.3 %gather_fusion.1 = bf16[32768,128]{1,0:T(8,128)(2,1)} fusion(bf16[128,3072]{0,1:T(8,128)(2,1)S(1)} %all_gather.14, s32[32768]{0:T(1024)S(1)} %broadcast_clamp_fusion), kind=kCustom, calls=%fused_computation.1 | custom fusion | bytes 16908288 | tf_op jit(solution)/shard_map/jit(_take)/gather | solution.py:42
  222.9 0.0 copy-done.2
  222.9 13.4 %multiply_reduce_fusion = bf16[128,2048]{0,1:T(8,128)(2,1)} fusion(f32[4,4,2048]{2,1,0:T(4,128)S(1)} %bitcast.39, bf16[128,4,4,2048]{0,3,2,1:T(8,128)(2,1)} %bitcast.35, pred[4,4,2048]{2,1,0:T(4,128)(4,1)S(1)} %compare_and_fusion), kind=kLoop, calls=%fused_computation.2 | loop fusion | flops 16515072 | bytes 9076736 | tf_op jit(solution)/shard_map/reduce_sum | solution.py:46
  236.3 0.0 all-gather.8.cloned.1.call-update
  236.3 44.8 %all-gather.8.cloned.1.call-done = bf16[512,2048]{0,1:T(8,128)(2,1)} async-done(((bf16[128,2048]{0,1:T(8,128)(2,1)}), bf16[512,2048]{0,1:T(8,128)(2,1)}) %all-gather.8.cloned.1.call-update) | async-done | bytes 2097168 | tf_op jit(solution)/shard_map/all_gather | solution.py:48
  281.2 6.1 %fusion.7 = bf16[1,512,1024]{2,1,0:T(8,128)(2,1)} fusion(bf16[512,2048]{0,1:T(8,128)(2,1)} %all-gather.8.cloned.1.call-done, bf16[2048,1024]{1,0:T(8,128)(2,1)} %param.15), kind=kOutput, calls=%fused_computation.10 | convolution fusion | flops 2148007936 | bytes 7340032 | tf_op jit(solution)/shard_map/dot_general | solution.py:47
  (4 shorter events, 0.0 us)
Async XLA Ops:
  6.5 52.2 %copy-start = (bf16[3,4,256,256]{3,2,1,0:T(8,128)(2,1)S(1)}, bf16[3,4,256,256]{3,2,1,0:T(8,128)(2,1)}, u32[]{:S(2)}) copy-start(bf16[3,4,256,256]{3,2,1,0:T(8,128)(2,1)} %param.9) | copy-start | bytes 4718596
  6.5 36.3 %copy-start.1 = (s32[1,4,4,2048]{3,2,1,0:T(4,128)S(1)}, s32[1,4,4,2048]{3,2,1,0:T(4,128)}, u32[]{:S(2)}) copy-start(s32[1,4,4,2048]{3,2,1,0:T(4,128)} %param.13) | copy-start | bytes 393220
  6.5 36.5 %copy-start.3 = (s32[3,4]{1,0:T(4,128)S(1)}, s32[3,4]{1,0:T(4,128)}, u32[]{:S(2)}) copy-start(s32[3,4]{1,0:T(4,128)} %param.11) | copy-start | bytes 148
  6.5 33.1 %all-gather.4.cloned.1.call-start = ((), (), s32[]{:S(2)}) async-start(), calls=%async_computation.1 | async-start | bytes 1310720 | tf_op jit(solution)/shard_map/all_gather | solution.py:20
  8.5 50.2 %all-gather.6.cloned.1.call-start = ((), (), s32[]{:S(2)}) async-start(), calls=%async_computation.2 | async-start | bytes 1310720 | tf_op jit(solution)/shard_map/all_gather | solution.py:22
  42.5 56.5 %reduce-scatter.2.cloned.1.call-start = ((), (), s32[]{:S(2)}) async-start(), calls=%async_computation.3 | async-start | bytes 1966080 | tf_op jit(solution)/shard_map/reduce_scatter | solution.py:29
  63.5 217.7 %all-gather.8.cloned.1.call-start = ((), (), s32[]{:S(2)}) async-start(), calls=%async_computation.4 | async-start | bytes 2621440 | tf_op jit(solution)/shard_map/all_gather | solution.py:48
  108.6 114.3 %copy-start.2 = (f32[1,4,4,2048]{3,2,1,0:T(4,128)S(1)}, f32[1,4,4,2048]{3,2,1,0:T(4,128)}, u32[]{:S(2)}) copy-start(f32[1,4,4,2048]{3,2,1,0:T(4,128)} %param.14) | copy-start | bytes 393220
Sparse Core Ops, SparseCore 0:
  8.9 30.6 all-gather.3
  42.6 16.0 all-gather.5
  63.6 35.4 reduce-scatter.1
  236.5 44.6 all-gather.7
where the time goes:
time: 294 us
  waiting for transfers between devices  126 us (43%)
  local copies, waits for them, and re-layouts  119 us (40%)
  other arithmetic  16.4 us (6%)
  between operations  13.2 us (4%)
  matrix products  10.8 us (4%)
  blocking collectives  8.58 us (3%)
    gather x1, local copies, waits for them, and re-layouts, shards(): jnp.take(layers, flat, axis=1).astype(jnp.float32)  114 us
    all_gather x1, waiting for transfers between devices, shards(): lax.all_gather(pupil, 'col', axis=0, tiled=True)  44.8 us
    reduce_scatter x1, waiting for transfers between devices, shards(): lax.psum_scatter(summed.reshape(lax.axis_size('col') * frame_share, rows_...  35.2 us
    all_gather x1, waiting for transfers between devices, shards(): partial_value = lax.all_gather(mine, 'col', axis=1, tiled=True)  30.3 us
    all_gather x1, waiting for transfers between devices, shards(): chosen = lax.all_gather(picked, ('row', 'dir'), axis=0, tiled=True)  15.6 us
    reduce_sum x1, other arithmetic, shards(): jnp.sum(values * trace_weight[0][None], axis=(1, 2)).astype(jnp.bfloat16)  13.4 us
    all_gather x1, blocking collectives, shards(): layers = lax.all_gather(layer_block, ('row', 'dir'), axis=1, tiled=True)  8.58 us
    dot_general x1, matrix products, shards(): jnp.dot(lax.all_gather(pupil, 'col', axis=0, tiled=True), fitting, prefer...  6.14 us
  transfers between devices with their start and end apart: 4, of which 4 were waited for; matrix products, arithmetic and copies ran while one was open for 1% of the time, Pallas kernels for 0%

commit v1 on v0

--- a/solution.py
+++ b/solution.py
@@ -17,7 +17,13 @@
     owners = lax.dynamic_slice_in_dim(tile_owner, lax.axis_index("col") * slots_here, slots_here, 0)
     share = frames // lax.axis_size(("row", "dir"))
     mine = lax.dynamic_slice_in_dim(slopes_in, lax.axis_index(("row", "dir")) * share, share, 0)
-    partial_value = lax.all_gather(mine, "col", axis=1, tiled=True)
+    devices = lax.axis_size("col")
+    held, blocks = (mine, [mine])
+    for _ in range(devices - 1):
+        held = lax.ppermute(held, "col", [(i, (i + 1) % devices) for i in range(devices)])
+        blocks.insert(0, held)
+    ravelled = jnp.concatenate(blocks, axis=1)
+    partial_value = jnp.roll(ravelled, (lax.axis_index("col") + 1) * mine.shape[1], axis=1)
     picked = jnp.take(partial_value.reshape(share, -1, tile_size), owners, axis=1)
     chosen = lax.all_gather(picked, ("row", "dir"), axis=0, tiled=True)
     columns = jnp.arange(rank_cols, dtype=jnp.int32) // RB

time: 294 us -> 291 us (0.990)
  waiting for transfers between devices: 126 us -> 119 us
  starting transfers between devices: 0.13 us -> 3.2 us
    all_gather x1 -> x0, waiting for transfers between devices: 30.3 us -> none  [shards(): partial_value = lax.all_gather(mine, 'col', axis=1, tiled=True)]
    ppermute x0 -> x3, waiting for transfers between devices: none -> 25.3 us  [shards(): lax.ppermute(held, 'col', [(i, (i + 1) % devices) for i in range(devices)])]
    ppermute x0 -> x3, starting transfers between devices: none -> 3.11 us  [shards(): lax.ppermute(held, 'col', [(i, (i + 1) % devices) for i in range(devices)])]
  transfers between devices with their start and end apart: 4 -> 6, of which waited for: 4 -> 6; matrix products, arithmetic and copies ran while one was open for 1% -> 1% of each run, Pallas kernels for 0% -> 0%
where the time goes in v1:
time: 291 us
  local copies, waits for them, and re-layouts  119 us (41%)
  waiting for transfers between devices  119 us (41%)
  other arithmetic  16.4 us (6%)
  between operations  13.3 us (5%)
  matrix products  10.8 us (4%)
  blocking collectives  8.58 us (3%)
  starting transfers between devices  3.2 us (1%)
    gather x1, local copies, waits for them, and re-layouts, shards(): jnp.take(layers, flat, axis=1).astype(jnp.float32)  114 us
    all_gather x1, waiting for transfers between devices, shards(): lax.all_gather(pupil, 'col', axis=0, tiled=True)  44.8 us
    reduce_scatter x1, waiting for transfers between devices, shards(): lax.psum_scatter(summed.reshape(lax.axis_size('col') * frame_share, rows_...  35.2 us
    ppermute x3, waiting for transfers between devices, shards(): lax.ppermute(held, 'col', [(i, (i + 1) % devices) for i in range(devices)])  25.3 us
    all_gather x1, waiting for transfers between devices, shards(): chosen = lax.all_gather(picked, ('row', 'dir'), axis=0, tiled=True)  14 us
    reduce_sum x1, other arithmetic, shards(): jnp.sum(values * trace_weight[0][None], axis=(1, 2)).astype(jnp.bfloat16)  13.4 us
    all_gather x1, blocking collectives, shards(): layers = lax.all_gather(layer_block, ('row', 'dir'), axis=1, tiled=True)  8.58 us
    dot_general x1, matrix products, shards(): jnp.dot(lax.all_gather(pupil, 'col', axis=0, tiled=True), fitting, prefer...  6.14 us
  transfers between devices with their start and end apart: 6, of which 6 were waited for; matrix products, arithmetic and copies ran while one was open for 1% of the time, Pallas kernels for 0%

profile of v1, /device:TPU:0, one launch (start us, length us, event | category | flops | bytes accessed | tf_op | source)
XLA Modules:
  0.0 290.9 jit_solution(10171082950441653292)
XLA Ops:
  6.5 0.0 copy-start
  6.5 0.0 all-gather.3.cloned.1.call-start
  6.5 1.1 constant_dynamic-slice_fusion.1
  7.6 0.2 copy.14
  7.8 3.1 %collective-permute-start = (bf16[128,1024]{0,1:T(8,128)(2,1)S(1)}, bf16[128,1024]{0,1:T(8,128)(2,1)S(1)}, u32[]{:S(2)}, u32[]{:S(2)}) collective-permute-start(bf16[128,1024]{0,1:T(8,128)(2,1)S(1)} %copy.14), channel_id=1, source_target_pairs={{0,4},{4,8},{8,12},{12,0},{1,5},{5,9},{9,13},{13,1},{2,6},{6,10},{... | collective-permute-start | bytes 786440 | tf_op jit(solution)/shard_map/ppermute | solution.py:23
  10.9 8.3 %collective-permute-done = bf16[128,1024]{0,1:T(8,128)(2,1)S(1)} collective-permute-done((bf16[128,1024]{0,1:T(8,128)(2,1)S(1)}, bf16[128,1024]{0,1:T(8,128)(2,1)S(1)}, u32[]{:S(2)}, u32[]{:S(2)}) %collective-permute-start) | collective-permute-done | bytes 262176 | tf_op jit(solution)/shard_map/ppermute | solution.py:23
  19.2 0.0 collective-permute-start.1
  19.2 9.3 %collective-permute-done.1 = bf16[128,1024]{0,1:T(8,128)(2,1)S(1)} collective-permute-done((bf16[128,1024]{0,1:T(8,128)(2,1)S(1)}, bf16[128,1024]{0,1:T(8,128)(2,1)S(1)}, u32[]{:S(2)}, u32[]{:S(2)}) %collective-permute-start.1) | collective-permute-done | bytes 262176 | tf_op jit(solution)/shard_map/ppermute | solution.py:23
  28.5 0.0 collective-permute-start.2
  28.5 0.7 compare_and_fusion.1
  29.3 7.7 %collective-permute-done.2 = bf16[128,1024]{0,1:T(8,128)(2,1)S(1)} collective-permute-done((bf16[128,1024]{0,1:T(8,128)(2,1)S(1)}, bf16[128,1024]{0,1:T(8,128)(2,1)S(1)}, u32[]{:S(2)}, u32[]{:S(2)}) %collective-permute-start.2) | collective-permute-done | bytes 262176 | tf_op jit(solution)/shard_map/ppermute | solution.py:23
  37.3 0.1 constant_dynamic-slice_fusion
  37.3 0.0 copy-start.1
  37.4 0.0 copy-start.3
  37.4 1.3 copy.12
  38.7 1.8 gather_fusion
  40.5 0.8 select_bitcast_fusion
  41.3 0.0 all-gather.3.cloned.1.call-update
  41.3 0.0 reduce-scatter.2.cloned.1.call-start
  41.3 0.1 add.80
  41.4 0.2 add.91
  41.6 0.0 copy-done.1
  41.6 0.2 squeeze.6
  41.8 0.0 copy-done.3
  41.8 0.1 broadcast_compare_fusion
  41.9 14.0 %all-gather.3.cloned.1.call-done = bf16[512,4,256]{2,0,1:T(8,128)(2,1)} async-done(((bf16[128,4,256]{2,0,1:T(8,128)(2,1)}), bf16[512,4,256]{2,0,1:T(8,128)(2,1)}) %all-gather.3.cloned.1.call-update) | async-done | bytes 1048592 | tf_op jit(solution)/shard_map/all_gather | solution.py:28
  55.9 0.0 copy-done
  55.9 4.7 %fusion.1 = f32[3,512,256,1]{1,2,3,0:T(8,128)} fusion(bf16[3,4,256,256]{3,2,1,0:T(8,128)(2,1)S(1)} %copy-done, pred[3,4,256]{2,1,0:T(4,128)(4,1)S(1)} %broadcast_compare_fusion, bf16[3,4,256,256]{3,2,1,0:T(8,128)(2,1)} %param.10, bf16[512,4,256]{2,0,1:T(8,128)(2,1)} %all-gather.3.cloned.1.call-done), kind=kOutput, calls=%fused_computation.5 | convolution fusion | flops 1613758464 | bytes 5770240 | tf_op jit(solution)/shard_map/ikfr,iknr->fin/dot_general | solution.py:34
  60.6 0.0 reduce-scatter.2.cloned.1.call-update
  60.6 0.0 all-gather.5.cloned.1.call-start
  60.7 0.2 compare_select_fusion
  60.9 0.2 compare_and_fusion
  61.1 35.2 %reduce-scatter.2.cloned.1.call-done = f32[128,768]{0,1:T(8,128)} async-done(((f32[512,768]{0,1:T(8,128)}), f32[128,768]{0,1:T(8,128)}) %reduce-scatter.2.cloned.1.call-update) | async-done | bytes 393232 | tf_op jit(solution)/shard_map/reduce_scatter | solution.py:35
  96.2 1.0 convert_element_type.17
  97.2 8.6 %all_gather.10 = bf16[128,3072]{0,1:T(8,128)(2,1)S(1)} all-gather(bf16[128,768]{0,1:T(8,128)(2,1)S(1)} %convert_element_type.17), channel_id=1, replica_groups=mesh['grp'=2,'col'=4,'row'=2,'dir'=2] {'row','dir'}, dimensions={1}, use_global_device_ids=true | all-gather | bytes 983040 | tf_op jit(solution)/shard_map/all_gather | solution.py:41
  105.8 0.0 copy-start.2
  105.8 114.2 %gather_fusion.1 = bf16[32768,128]{1,0:T(8,128)(2,1)} fusion(bf16[128,3072]{0,1:T(8,128)(2,1)S(1)} %all_gather.10, s32[32768]{0:T(1024)S(1)} %broadcast_clamp_fusion), kind=kCustom, calls=%fused_computation.1 | custom fusion | bytes 16908288 | tf_op jit(solution)/shard_map/jit(_take)/gather | solution.py:48
  220.0 0.0 copy-done.2
  220.0 13.4 %multiply_reduce_fusion = bf16[128,2048]{0,1:T(8,128)(2,1)} fusion(f32[4,4,2048]{2,1,0:T(4,128)S(1)} %bitcast.39, bf16[128,4,4,2048]{0,3,2,1:T(8,128)(2,1)} %bitcast.35, pred[4,4,2048]{2,1,0:T(4,128)(4,1)S(1)} %compare_and_fusion), kind=kLoop, calls=%fused_computation.2 | loop fusion | flops 16515072 | bytes 9076736 | tf_op jit(solution)/shard_map/reduce_sum | solution.py:52
  233.4 0.0 all-gather.5.cloned.1.call-update
  233.4 44.8 %all-gather.5.cloned.1.call-done = bf16[512,2048]{0,1:T(8,128)(2,1)} async-done(((bf16[128,2048]{0,1:T(8,128)(2,1)}), bf16[512,2048]{0,1:T(8,128)(2,1)}) %all-gather.5.cloned.1.call-update) | async-done | bytes 2097168 | tf_op jit(solution)/shard_map/all_gather | solution.py:54
  278.2 6.1 %fusion.7 = bf16[1,512,1024]{2,1,0:T(8,128)(2,1)} fusion(bf16[512,2048]{0,1:T(8,128)(2,1)} %all-gather.5.cloned.1.call-done, bf16[2048,1024]{1,0:T(8,128)(2,1)} %param.15), kind=kOutput, calls=%fused_computation.10 | convolution fusion | flops 2148007936 | bytes 7340032 | tf_op jit(solution)/shard_map/dot_general | solution.py:53
  (12 shorter events, 0.3 us)
Async XLA Ops:
  6.5 49.4 %copy-start = (bf16[3,4,256,256]{3,2,1,0:T(8,128)(2,1)S(1)}, bf16[3,4,256,256]{3,2,1,0:T(8,128)(2,1)}, u32[]{:S(2)}) copy-start(bf16[3,4,256,256]{3,2,1,0:T(8,128)(2,1)} %param.9) | copy-start | bytes 4718596
  6.5 49.4 %all-gather.3.cloned.1.call-start = ((), (), s32[]{:S(2)}) async-start(), calls=%async_computation.1 | async-start | bytes 1310720 | tf_op jit(solution)/shard_map/all_gather | solution.py:28
  7.8 11.4 %collective-permute-start = (bf16[128,1024]{0,1:T(8,128)(2,1)S(1)}, bf16[128,1024]{0,1:T(8,128)(2,1)S(1)}, u32[]{:S(2)}, u32[]{:S(2)}) collective-permute-start(bf16[128,1024]{0,1:T(8,128)(2,1)S(1)} %copy.14), channel_id=1, source_target_pairs={{0,4},{4,8},{8,12},{12,0},{1,5},{5,9},{9,13},{13,1},{2,6},{6,10},{... | collective-permute-start | bytes 786440 | tf_op jit(solution)/shard_map/ppermute | solution.py:23
  19.2 9.3 %collective-permute-start.1 = (bf16[128,1024]{0,1:T(8,128)(2,1)S(1)}, bf16[128,1024]{0,1:T(8,128)(2,1)S(1)}, u32[]{:S(2)}, u32[]{:S(2)}) collective-permute-start(bf16[128,1024]{0,1:T(8,128)(2,1)S(1)} %collective-permute-done), channel_id=1, source_target_pairs={{0,4},{4,8},{8,12},{12,0},{1,5},{5,9},{9,13},{13,1},{2,6},{6,10},{... | collective-permute-start | bytes 786440 | tf_op jit(solution)/shard_map/ppermute | solution.py:23
  28.5 8.4 %collective-permute-start.2 = (bf16[128,1024]{0,1:T(8,128)(2,1)S(1)}, bf16[128,1024]{0,1:T(8,128)(2,1)S(1)}, u32[]{:S(2)}, u32[]{:S(2)}) collective-permute-start(bf16[128,1024]{0,1:T(8,128)(2,1)S(1)} %collective-permute-done.1), channel_id=1, source_target_pairs={{0,4},{4,8},{8,12},{12,0},{1,5},{5,9},{9,13},{13,1},{2,6},{6,10},{... | collective-permute-start | bytes 786440 | tf_op jit(solution)/shard_map/ppermute | solution.py:23
  37.3 4.3 %copy-start.1 = (s32[1,4,4,2048]{3,2,1,0:T(4,128)S(1)}, s32[1,4,4,2048]{3,2,1,0:T(4,128)}, u32[]{:S(2)}) copy-start(s32[1,4,4,2048]{3,2,1,0:T(4,128)} %param.13) | copy-start | bytes 393220
  37.4 4.5 %copy-start.3 = (s32[3,4]{1,0:T(4,128)S(1)}, s32[3,4]{1,0:T(4,128)}, u32[]{:S(2)}) copy-start(s32[3,4]{1,0:T(4,128)} %param.11) | copy-start | bytes 148
  41.3 54.9 %reduce-scatter.2.cloned.1.call-start = ((), (), s32[]{:S(2)}) async-start(), calls=%async_computation.2 | async-start | bytes 1966080 | tf_op jit(solution)/shard_map/reduce_scatter | solution.py:35
  60.6 217.6 %all-gather.5.cloned.1.call-start = ((), (), s32[]{:S(2)}) async-start(), calls=%async_computation.3 | async-start | bytes 2621440 | tf_op jit(solution)/shard_map/all_gather | solution.py:54
  105.8 114.2 %copy-start.2 = (f32[1,4,4,2048]{3,2,1,0:T(4,128)S(1)}, f32[1,4,4,2048]{3,2,1,0:T(4,128)}, u32[]{:S(2)}) copy-start(f32[1,4,4,2048]{3,2,1,0:T(4,128)} %param.14) | copy-start | bytes 393220
Sparse Core Ops, SparseCore 0:
  41.4 14.4 all-gather.2
  60.7 35.4 reduce-scatter.1
  233.5 44.6 all-gather.4
